TPU v7x, 32 devices: a whole 2x2x4 slice. The times are simulated.
32 devices in a mesh: tmpl: 2 (over core), row: 4 (over z), col: 4 (over y, x).
Axes of the slice: x: 2, y: 2, z: 4, core: 2. Of those that a mesh axis runs over, the one named last changes fastest.
Arguments:
- template_pair: bfloat16 [2, 512, 64, 512], P('tmpl', 'row', None, 'col'), may hold values from -6 to 6
- trunk: bfloat16 [512, 128, 512], P('row', None, 'col'), may hold values from -6 to 6
- coverage: int32 [2, 512], replicated, may hold values from 0 to 1, as said below
- chain_ids: int32 [512], replicated, may hold values from 0 to 3, never falling along the last dimension, each value on 1 to 256 neighbouring positions
- chain_vec: float32 [64], replicated, may hold values from -4 to 4
- trunk_weights: bfloat16 [64, 128], replicated, may hold values from -0.5 to 0.5
- proj_weights: bfloat16 [2, 5, 64, 64], replicated, may hold values from -0.75 to 0.75
- out_weights: bfloat16 [2, 64, 64], replicated, may hold values from -0.75 to 0.75
- final_weights: bfloat16 [128, 64], replicated, may hold values from -0.75 to 0.75
Outputs:
- trunk_out: bfloat16 [512, 128, 512], P('row', None, 'col')
Inputs may be any that keep to these rules, and one draw needn't show every extreme that they name: coverage[t, i] is 1 where template t covers token i, else 0; how densely a template covers tokens is drawn anew for each block of 128 consecutive tokens. `chain_ids`: chain ids never fall along the tokens.
All inputs are finite; a program needn't handle non-finite values.
Results may differ from a plain program's by a relative error of at most 0.008.
Values may be sent and summed in bfloat16 or wider, within the bound.
No kernel may reach another device: no remote copies, remote signals or barrier semaphores. Data moves between devices by JAX's collectives and lax.ppermute only.
A program may use at most 128 MiB of HBM per device.

v0:
```python
import functools

import jax
import jax.numpy as jnp
from jax import lax
from jax.experimental import pallas as pl
from jax.experimental.pallas import tpu as pltpu
from jax.sharding import PartitionSpec as P

epsilon = 1e-05
GROUP = 16
F32 = jnp.float32
BF16 = jnp.bfloat16


def sigmoid(x):
    return 0.5 * jnp.tanh(0.5 * x) + 0.5


def norm_rows(x):
    scale = 1.0 / x.shape[0]
    centred = x - jnp.sum(x, axis=0, keepdims=True) * scale
    spread = jnp.sum(centred * centred, axis=0, keepdims=True) * scale
    return centred * lax.rsqrt(spread + epsilon)


def project_rows(weights, rows):
    wide = jnp.concatenate(rows, axis=1)
    out = jnp.dot(weights, wide, preferred_element_type=F32)
    cols = rows[0].shape[1]
    return [out[:, n * cols : (n + 1) * cols] for n in range(len(rows))]


def emit_gated(reps, masks, first, weights_ref, gate_ref, scratch):
    channels = reps[0].shape[0]
    normed = [norm_rows(rep).astype(BF16) for rep in reps]
    for half in range(0, len(reps), 2):
        pieces = project_rows(weights_ref[...], normed[half : half + 2])
        for n, piece in enumerate(pieces):
            p = [piece[k * channels : (k + 1) * channels] for k in range(5)]
            at = first + half + n
            rows = pl.ds(pl.multiple_of(at * (channels + PAD), 8), channels)
            mask = masks[half + n]
            scratch[0, rows, :] = mask * sigmoid(p[0]) * p[1]
            scratch[1, rows, :] = mask * sigmoid(p[2]) * p[3]
            gate_ref[at] = sigmoid(p[4]).astype(gate_ref.dtype)


def store_by_channel(scratch, pair_ref):
    slots, _, per_slot = pair_ref.shape[:3]
    channels = slots * per_slot
    for side in range(2):
        for channel in range(channels):
            rows = scratch[side, pl.ds(channel, GROUP, stride=channels + PAD), :]
            pair_ref[channel // per_slot, side, channel % per_slot] = rows.astype(BF16)


STEP = 16
PAD = 8


def block_mask(counts_ref, width, unit):
    template = lax.axis_index("tmpl")
    lanes = lax.broadcasted_iota(jnp.int32, (1, width), 1)
    owners = width // unit
    first = lax.axis_index("col") * owners
    mask = jnp.zeros((1, width), F32)
    for owner in range(owners):
        low = owner * unit
        inside = (lanes >= low) & (lanes < low + counts_ref[template, first + owner])
        mask = jnp.where(inside, 1.0, mask)
    return mask


def selection(cover, unit):
    width = cover.shape[1]
    source = lax.broadcasted_iota(jnp.int32, (width, width), 0)
    target = lax.broadcasted_iota(jnp.int32, (width, width), 1)
    upper = ((source <= target) & (source // unit == target // unit)).astype(F32).astype(BF16)
    wide = jnp.broadcast_to(cover, (GROUP, width)).astype(BF16)
    ranks = jnp.dot(wide, upper, preferred_element_type=F32)[:1].astype(jnp.int32)
    slots = target[:1] // unit * unit + ranks - 1
    return jnp.where((source == slots) & (cover > 0.5), 1.0, 0.0)


def template_row(rows, template):
    out = rows[:1]
    for t in range(1, rows.shape[0]):
        out = jnp.where(template == t, rows[t : t + 1], out)
    return out


def pre_kernel(unit, cover_ref, chain_ref, counts_ref, tp_hbm, trunk_hbm, cover_all_ref, chain_all_ref, chain_vec_ref,
               trunk_weights_ref, weights_ref, pair_ref, rep_ref, gate_ref,
               scratch, tp_buffer, trunk_buffer, order, pick, sems):
    step_id = pl.program_id(0)
    base = step_id * GROUP
    cols = tp_buffer.shape[3]
    channels = tp_buffer.shape[2]
    template = lax.axis_index("tmpl")
    row_start = lax.axis_index("row") * unit
    col_start = pl.multiple_of(lax.axis_index("col") * cols, cols)
    slot = lax.rem(step_id, 2)

    def copies(group, into):
        out = []
        for n in range(GROUP):
            row = order[group * GROUP + n]
            out.append(pltpu.make_async_copy(tp_hbm.at[0, row], tp_buffer.at[into, n], sems.at[into, 0, n]))
            out.append(pltpu.make_async_copy(trunk_hbm.at[row], trunk_buffer.at[into, n], sems.at[into, 1, n]))
        return out

    @pl.when(step_id == 0)
    def _():
        def place(row, taken):
            covered = cover_ref[template, row_start + row]
            order[jnp.where(covered > 0, taken, unit - 1 - (row - taken))] = row
            return taken + covered

        lax.fori_loop(0, unit, place, 0, unroll=8)
        for copy in copies(0, 0):
            copy.start()
        cover = template_row(cover_all_ref[:, pl.ds(col_start, cols)].astype(F32), template)
        pick[...] = jnp.transpose(selection(cover, unit)).astype(BF16)

    @pl.when(step_id + 1 < pl.num_programs(0))
    def _():
        for copy in copies(step_id + 1, 1 - slot):
            copy.start()

    for copy in copies(step_id, slot):
        copy.wait()

    trunk_weights = trunk_weights_ref[...]
    weight_sums = jnp.sum(trunk_weights.astype(F32), axis=1, keepdims=True)
    chain_cols = chain_all_ref[:, pl.ds(col_start, cols)]
    col_mask = block_mask(counts_ref, cols, unit)
    row_count = counts_ref[template, lax.axis_index("row")]

    def body(step, carry):
        first = step * STEP
        raw, masks = [], []
        rows = [trunk_buffer[slot, first + n] for n in range(STEP)]
        projected = []
        for half in range(0, STEP, 2):
            projected += project_rows(trunk_weights, rows[half : half + 2])
        for n in range(STEP):
            at = first + n
            values = rows[n].astype(F32)
            scale = 1.0 / values.shape[0]
            centre = jnp.sum(values, axis=0, keepdims=True) * scale
            centred = values - centre
            spread = jnp.sum(centred * centred, axis=0, keepdims=True) * scale
            trunk_proj = (projected[n] - weight_sums * centre) * lax.rsqrt(spread + epsilon)
            same = (chain_cols == chain_ref[row_start + order[base + at]]).astype(F32)
            raw.append((tp_buffer[slot, at].astype(F32) + same * chain_vec_ref[...] + trunk_proj).astype(BF16))
            masks.append(jnp.where(base + at < row_count, col_mask, 0.0))
        picked = jnp.dot(jnp.concatenate(raw, axis=0), pick[...], preferred_element_type=F32)
        reps = [picked[n * channels : (n + 1) * channels] for n in range(STEP)]
        for n in range(STEP):
            rep_ref[first + n] = reps[n].astype(BF16)
        emit_gated(reps, masks, first, weights_ref, gate_ref, scratch)
        return carry

    lax.fori_loop(0, GROUP // STEP, body, 0)
    store_by_channel(scratch, pair_ref)


def load_tri(tri_ref, tri_scratch):
    channels = tri_ref.shape[0]
    scale = 1.0 / channels
    half = GROUP // 2
    for part in range(2):
        rows = slice(part * half, (part + 1) * half)
        total = jnp.zeros((half, tri_ref.shape[2]), F32)
        for channel in range(channels):
            total += tri_ref[channel].astype(F32)[rows]
        centre = total * scale
        total = jnp.zeros_like(total)
        for channel in range(channels):
            centred = tri_ref[channel].astype(F32)[rows] - centre
            total += centred * centred
        inverse = lax.rsqrt(total * scale + epsilon)
        for channel in range(channels):
            at = channel * (GROUP + PAD) + part * half
            tri_scratch[at : at + half, :] = (
                tri_ref[channel].astype(F32)[rows] - centre
            ) * inverse


def updated_rows(first, tri_scratch, rep_ref, gate_ref, out_weights_ref):
    channels = rep_ref.shape[1]
    normed = [
        tri_scratch[pl.ds(first + n, channels, stride=GROUP + PAD), :].astype(BF16) for n in range(STEP)
    ]
    projected = []
    for half in range(0, STEP, 2):
        projected += project_rows(out_weights_ref[...], normed[half : half + 2])
    return [
        (rep_ref[first + n].astype(F32) + gate_ref[first + n].astype(F32) * projected[n]).astype(BF16)
        for n in range(STEP)
    ]


def mid_kernel(unit, counts_ref, tri_ref, rep_in_ref, gate_in_ref, out_weights_ref, weights_ref,
               pair_ref, rep_ref, gate_ref, scratch, tri_scratch):
    base = pl.program_id(0) * GROUP
    load_tri(tri_ref, tri_scratch)
    col_mask = block_mask(counts_ref, rep_ref.shape[2], unit)
    row_count = counts_ref[lax.axis_index("tmpl"), lax.axis_index("row")]

    def body(step, carry):
        first = step * STEP
        rows = updated_rows(first, tri_scratch, rep_in_ref, gate_in_ref, out_weights_ref)
        masks = []
        for n in range(STEP):
            rep_ref[first + n] = rows[n]
            masks.append(jnp.where(base + first + n < row_count, col_mask, 0.0))
        emit_gated([row.astype(F32) for row in rows], masks, first, weights_ref, gate_ref, scratch)
        return carry

    lax.fori_loop(0, GROUP // STEP, body, 0)
    store_by_channel(scratch, pair_ref)


def last_kernel(tri_ref, rep_in_ref, gate_in_ref, out_weights_ref, pooled_ref, tri_scratch):
    load_tri(tri_ref, tri_scratch)

    def body(step, carry):
        first = step * STEP
        rows = updated_rows(first, tri_scratch, rep_in_ref, gate_in_ref, out_weights_ref)
        for n in range(STEP):
            pooled_ref[first + n] = norm_rows(rows[n].astype(F32)).astype(BF16)
        return carry

    lax.fori_loop(0, GROUP // STEP, body, 0)


def finish_kernel(unit, cover_ref, mine_ref, other_ref, trunk_ref, cover_all_ref, final_weights_ref, out_ref,
                  place, spread):
    step_id = pl.program_id(0)
    base = step_id * GROUP
    cols = out_ref.shape[2]
    channels = mine_ref.shape[1]
    template = lax.axis_index("tmpl")
    templates = (template, 1 - template)
    row_start = lax.axis_index("row") * unit
    col_start = pl.multiple_of(lax.axis_index("col") * cols, cols)
    cover_cols = cover_all_ref[:, pl.ds(col_start, cols)].astype(F32)
    covers = [template_row(cover_cols, t) for t in templates]

    @pl.when(step_id == 0)
    def _():
        def count(row, taken):
            out = []
            for k, t in enumerate(templates):
                covered = cover_ref[t, row_start + row]
                place[k, row] = jnp.where(covered > 0, taken[k], 0)
                out.append(taken[k] + covered)
            return tuple(out)

        lax.fori_loop(0, unit, count, (0,) * len(templates), unroll=8)
        for k in range(len(templates)):
            spread[k * cols : (k + 1) * cols, :] = selection(covers[k], unit).astype(BF16)

    def body(step, carry):
        first = step * STEP
        packed, counts = [], []
        for n in range(STEP):
            row = base + first + n
            parts = []
            count = jnp.zeros_like(covers[0])
            for k, (t, ref) in enumerate(zip(templates, (mine_ref, other_ref))):
                covered = cover_ref[t, row_start + row]
                value = ref[place[k, row]].astype(F32)
                parts.append(jnp.where(covered > 0, value, 0.0).astype(BF16))
                count += covers[k] * covered.astype(F32)
            packed.append(jnp.concatenate(parts, axis=1))
            counts.append(count)
        pooled = jnp.dot(jnp.concatenate(packed, axis=0), spread[...], preferred_element_type=F32)
        hidden = [
            jnp.maximum(pooled[n * channels : (n + 1) * channels] * (1.0 / jnp.maximum(counts[n], 1.0)), 0.0).astype(BF16)
            for n in range(STEP)
        ]
        for half in range(0, STEP, 2):
            for n, row in enumerate(project_rows(final_weights_ref[...], hidden[half : half + 2])):
                at = first + half + n
                out_ref[at] = (trunk_ref[at].astype(F32) + row).astype(BF16)
        return carry

    lax.fori_loop(0, GROUP // STEP, body, 0)


def gather_sides(rows_n, cols_n, unit, pair_ref, sides):
    height, width = pair_ref.shape[3:]

    @pl.when(pl.program_id(0) == 0)
    def _():
        if height < unit:
            sides[...] = jnp.zeros_like(sides)

    for side in range(2):
        for r in range(rows_n):
            for c in range(cols_n):
                sides[side, r * unit : r * unit + height, c * width : (c + 1) * width] = pair_ref[
                    r * cols_n + c, side, 0
                ]


def triangle_kernel(contract, rows_n, cols_n, unit, pair_ref, tri_ref, sides):
    gather_sides(rows_n, cols_n, unit, pair_ref, sides)
    out = lax.dot_general(
        sides[0], sides[1], (((contract,), (contract,)), ((), ())), preferred_element_type=F32
    )
    height, width = tri_ref.shape[2:]
    for r in range(rows_n):
        for c in range(cols_n):
            tri_ref[r * cols_n + c, 0] = out[
                r * unit : r * unit + height, c * width : (c + 1) * width
            ].astype(BF16)


def triangle(contract, rows_n, cols_n, unit, pairs, name):
    slots, _, per_slot, height, width = pairs.shape
    return pl.pallas_call(
        functools.partial(triangle_kernel, contract, rows_n, cols_n, unit),
        grid=(per_slot,),
        in_specs=[pl.BlockSpec((slots, 2, 1, height, width), lambda c: (0, 0, c, 0, 0))],
        out_specs=pl.BlockSpec((slots, 1, height, width), lambda c: (0, c, 0, 0)),
        out_shape=jax.ShapeDtypeStruct((slots, per_slot, height, width), BF16),
        scratch_shapes=[pltpu.VMEM((2, rows_n * unit, cols_n * width), BF16)],
        name=name,
    )(pairs)


SMEM = pl.BlockSpec(memory_space=pltpu.SMEM)
ANY = pl.BlockSpec(memory_space=pl.ANY)


def whole_block(array):
    zeros = (0,) * array.ndim
    return pl.BlockSpec(array.shape, lambda g: zeros)


def rows_block(*rest):
    zeros = (0,) * len(rest)
    return pl.BlockSpec((GROUP,) + rest, lambda g: (g,) + zeros)


def with_capacity(
    capacity,
    counts,
    template_pair,
    trunk,
    coverage,
    chain_ids,
    chain_vec,
    trunk_weights,
    proj_weights,
    out_weights,
    final_weights,
):
    unit, trunk_channels, tile_cols = trunk.shape
    channels = template_pair.shape[2]
    rows_n, cols_n = lax.axis_size("row"), lax.axis_size("col")
    slots = rows_n * cols_n
    per_slot = channels // slots
    grid = (pl.cdiv(capacity, GROUP),)
    stacked = proj_weights.reshape(2, 5 * channels, channels)
    chain_all = chain_ids[None]
    chain_column = chain_vec[:, None]

    pair_spec = pl.BlockSpec((slots, 2, per_slot, GROUP, tile_cols), lambda g: (0, 0, 0, g, 0))
    pair_shape = jax.ShapeDtypeStruct((slots, 2, per_slot, capacity, tile_cols), BF16)
    rep_spec = rows_block(channels, tile_cols)
    rep_shape = jax.ShapeDtypeStruct((capacity, channels, tile_cols), BF16)
    trunk_spec = rows_block(trunk_channels, tile_cols)
    tri_spec = pl.BlockSpec((channels, GROUP, tile_cols), lambda g: (0, g, 0))
    scratch = pltpu.VMEM((2, GROUP * (channels + PAD), tile_cols), F32)
    tri_scratch = pltpu.VMEM((channels * (GROUP + PAD), tile_cols), F32)
    gated_outs = dict(
        out_specs=[pair_spec, rep_spec, rep_spec], out_shape=[pair_shape, rep_shape, rep_shape]
    )

    def exchange(values):
        return lax.all_to_all(values, ("row", "col"), 0, 0, tiled=True)

    pairs, rep, gate = pl.pallas_call(
        functools.partial(pre_kernel, unit),
        grid=grid,
        in_specs=[
            SMEM,
            SMEM,
            SMEM,
            ANY,
            ANY,
            whole_block(coverage),
            whole_block(chain_all),
            whole_block(chain_column),
            whole_block(trunk_weights),
            whole_block(stacked[0]),
        ],
        scratch_shapes=[
            scratch,
            pltpu.VMEM((2, GROUP, channels, tile_cols), BF16),
            pltpu.VMEM((2, GROUP, trunk_channels, tile_cols), BF16),
            pltpu.SMEM((unit,), jnp.int32),
            pltpu.VMEM((tile_cols, tile_cols), BF16),
            pltpu.SemaphoreType.DMA((2, 2, GROUP)),
        ],
        name="pre",
        **gated_outs,
    )(coverage, chain_ids, counts, template_pair, trunk, coverage, chain_all, chain_column, trunk_weights, stacked[0])

    tri = exchange(triangle(1, rows_n, cols_n, unit, exchange(pairs), "outgoing"))
    pairs, rep, gate = pl.pallas_call(
        functools.partial(mid_kernel, unit),
        grid=grid,
        in_specs=[SMEM, tri_spec, rep_spec, rep_spec, whole_block(out_weights[0]), whole_block(stacked[1])],
        scratch_shapes=[scratch, tri_scratch],
        name="mid",
        **gated_outs,
    )(counts, tri.reshape(channels, capacity, tile_cols), rep, gate, out_weights[0], stacked[1])

    tri = exchange(triangle(0, rows_n, cols_n, unit, exchange(pairs), "incoming"))
    pooled = pl.pallas_call(
        last_kernel,
        grid=grid,
        in_specs=[tri_spec, rep_spec, rep_spec, whole_block(out_weights[1])],
        out_specs=rep_spec,
        out_shape=rep_shape,
        scratch_shapes=[tri_scratch],
        name="last",
    )(tri.reshape(channels, capacity, tile_cols), rep, gate, out_weights[1])

    other = lax.ppermute(pooled, "tmpl", [(0, 1), (1, 0)])
    return pl.pallas_call(
        functools.partial(finish_kernel, unit),
        grid=(unit // GROUP,),
        in_specs=[
            SMEM,
            whole_block(pooled),
            whole_block(pooled),
            trunk_spec,
            whole_block(coverage),
            whole_block(final_weights),
        ],
        out_specs=trunk_spec,
        out_shape=jax.ShapeDtypeStruct(trunk.shape, BF16),
        scratch_shapes=[pltpu.SMEM((2, unit), jnp.int32), pltpu.VMEM((2 * tile_cols, tile_cols), BF16)],
        name="finish",
    )(coverage, pooled, other, trunk, coverage, final_weights)


def per_device(template_pair, trunk, coverage, *rest):
    unit, _, tile_cols = trunk.shape
    templates, tokens = coverage.shape
    counts = jnp.sum(coverage.reshape(templates, tokens // unit, unit), axis=2)
    capacities = [unit]
    if unit == tile_cols and unit % 16 == 0:
        capacities = [unit * share // 16 for share in (12, 13, 14, 16)]
    args = (counts, template_pair, trunk, coverage) + rest
    if len(capacities) == 1:
        return with_capacity(unit, *args)
    most = jnp.max(counts)
    branch = sum((most > capacity).astype(jnp.int32) for capacity in capacities[:-1])
    return lax.switch(branch, [functools.partial(with_capacity, capacity) for capacity in capacities], *args)


def solution(mesh):
    in_specs = (
        P("tmpl", "row", None, "col"),
        P("row", None, "col"),
        P(),
        P(),
        P(),
        P(),
        P(),
        P(),
        P(),
    )
    out_specs = P("row", None, "col")
    return jax.shard_map(
        per_device, mesh=mesh, in_specs=in_specs, out_specs=out_specs, check_vma=False
    )
```

profile of v0, /device:TPU:0, one launch (start us, length us, event | category | flops | bytes accessed | tf_op | source)
XLA Modules:
  0.0 321.6 jit_solution(8073238574712466726)
XLA Ops:
  0.0 0.7 reshape.47
  0.7 0.1 reduce_sum.9
  0.8 0.6 reduce_max.9
  3.4 318.2 %conditional.1 = (bf16[128,128,128]{2,1,0:T(8,128)(2,1)}) conditional(s32[]{:T(128)} %clamp.3, (s32[512]{0:T(512)}, f32[64]{0:T(128)}, bf16[2,5,64,64]{3,2,1,0:T(8,128)(2,1)}, s32[2,512]{1,0:T(2,128)}, s32[2,4]{1,0:T(2,128)S(1)}, /*index=5*/bf16[1,128,64,128]{3,2,1,0:T(8,128)(2,1)}, bf16[128,128,128]{2,1,0:T(8,128)(2,1)}, ...), branch_computations={%region_2.0_spmd, %region_3.0_spmd, %region_4.0_spmd, %region_5.0_... | conditional | bytes 52806364 | solution.py:467
  3.4 1.6 fusion.1
  5.0 1.4 copy.15.chain_vec_ref
  6.4 14.1 %pre.5 = (bf16[16,2,4,104,128]{4,3,2,1,0:T(8,128)(2,1)}, bf16[104,64,128]{2,1,0:T(8,128)(2,1)}, bf16[104,64,128]{2,1,0:T(8,128)(2,1)}) custom-call(s32[2,512]{1,0:T(2,128)} %get-tuple-element.106.cover_ref.cover_all_ref, s32[512]{0:T(512)} %get-tuple-element.108.chain_ref, s32[2,4]{1,0:T(2,128)S(1)} %get-tuple-element.107.counts_ref, ...), custom_call_target="tpu_custom_call" | custom-call | tf_op jit(solution)/shard_map/cond/branch_1_fun/pre/pallas_call | solution.py:388
  20.5 85.9 %all_to_all.67.pair_ref = bf16[16,2,4,104,128]{4,3,2,1,0:T(8,128)(2,1)} all-to-all(bf16[16,2,4,104,128]{4,3,2,1,0:T(8,128)(2,1)} %get-tuple-element.114), channel_id=1, replica_groups=mesh['tmpl'=2,'row'=4,'col'=4] {'row','col'}, dimensions={0} | all-to-all | bytes 6815744 | tf_op jit(solution)/shard_map/cond/branch_1_fun/all_to_all | solution.py:386
  106.4 5.0 %outgoing.5 = bf16[16,4,104,128]{3,2,1,0:T(8,128)(2,1)} custom-call(bf16[16,2,4,104,128]{4,3,2,1,0:T(8,128)(2,1)} %all_to_all.67.pair_ref), custom_call_target="tpu_custom_call" | custom-call | tf_op jit(solution)/shard_map/cond/branch_1_fun/outgoing/pallas_call | solution.py:325
  111.3 0.0 copy-start.13
  111.3 3.8 %all-to-all-start.5 = ((bf16[16,4,104,128]{3,2,1,0:T(8,128)(2,1)}), bf16[16,4,104,128]{3,2,1,0:T(8,128)(2,1)S(1)}, u32[]{:S(2)}, u32[]{:S(2)}) async-start(bf16[16,4,104,128]{3,2,1,0:T(8,128)(2,1)} %outgoing.5), calls=%async_computation.5 | async-start | bytes 3407872 | tf_op jit(solution)/shard_map/cond/branch_1_fun/all_to_all | solution.py:386
  115.2 0.0 copy-done.13
  115.2 0.6 slice_bitcast_fusion.2
  115.8 35.1 %all-to-all-done.5 = bf16[16,4,104,128]{3,2,1,0:T(8,128)(2,1)S(1)} async-done(((bf16[16,4,104,128]{3,2,1,0:T(8,128)(2,1)}), bf16[16,4,104,128]{3,2,1,0:T(8,128)(2,1)S(1)}, u32[]{:S(2)}, u32[]{:S(2)}) %all-to-all-start.5) | async-done | bytes 1703968 | tf_op jit(solution)/shard_map/cond/branch_1_fun/all_to_all | solution.py:386
  150.9 0.0 copy-start.2
  150.9 1.2 copy-done.2
  152.2 10.9 %mid.5 = (bf16[16,2,4,104,128]{4,3,2,1,0:T(8,128)(2,1)}, bf16[104,64,128]{2,1,0:T(8,128)(2,1)}, bf16[104,64,128]{2,1,0:T(8,128)(2,1)}) custom-call(s32[2,4]{1,0:T(2,128)S(1)} %get-tuple-element.107.counts_ref, bf16[64,104,128]{2,1,0:T(8,128)(2,1)} %bitcast.44, bf16[104,64,128]{2,1,0:T(8,128)(2,1)} %get-tuple-element.115.rep_in_ref, ...), custom_call_target="tpu_custom_call" | custom-call | tf_op jit(solution)/shard_map/cond/branch_1_fun/mid/pallas_call | solution.py:416
  163.1 84.9 %all_to_all.68.pair_ref = bf16[16,2,4,104,128]{4,3,2,1,0:T(8,128)(2,1)} all-to-all(bf16[16,2,4,104,128]{4,3,2,1,0:T(8,128)(2,1)} %get-tuple-element.118), channel_id=1, replica_groups=mesh['tmpl'=2,'row'=4,'col'=4] {'row','col'}, dimensions={0} | all-to-all | bytes 6815744 | tf_op jit(solution)/shard_map/cond/branch_1_fun/all_to_all | solution.py:386
  248.0 5.0 %incoming.5 = bf16[16,4,104,128]{3,2,1,0:T(8,128)(2,1)} custom-call(bf16[16,2,4,104,128]{4,3,2,1,0:T(8,128)(2,1)} %all_to_all.68.pair_ref), custom_call_target="tpu_custom_call" | custom-call | tf_op jit(solution)/shard_map/cond/branch_1_fun/incoming/pallas_call | solution.py:325
  253.0 44.8 %all_to_all.69 = bf16[16,4,104,128]{3,2,1,0:T(8,128)(2,1)} all-to-all(bf16[16,4,104,128]{3,2,1,0:T(8,128)(2,1)} %incoming.5), channel_id=1, replica_groups=mesh['tmpl'=2,'row'=4,'col'=4] {'row','col'}, dimensions={0} | all-to-all | bytes 3407872 | tf_op jit(solution)/shard_map/cond/branch_1_fun/all_to_all | solution.py:386
  297.8 0.0 copy-start.17
  297.8 0.0 copy-start.9
  297.8 7.7 %last.5.mine_ref = bf16[104,64,128]{2,1,0:T(8,128)(2,1)} custom-call(bf16[64,104,128]{2,1,0:T(8,128)(2,1)} %bitcast.45, bf16[104,64,128]{2,1,0:T(8,128)(2,1)} %get-tuple-element.119.rep_in_ref, bf16[104,64,128]{2,1,0:T(8,128)(2,1)} %get-tuple-element.120.gate_in_ref, bf16[64,64]{1,0:T(8,128)(2,1)} %get-tuple-element.201.out_weights_ref), custom_call_target="tpu_custom_call" | custom-call | tf_op jit(solution)/shard_map/cond/branch_1_fun/last/pallas_call | solution.py:426
  305.5 0.0 collective-permute-start.1
  305.5 0.0 copy-done.17
  305.5 0.7 copy.19.final_weights_ref
  306.2 3.1 collective-permute-done.1.other_ref
  309.3 0.0 copy-start.6
  309.3 1.2 copy-done.6
  310.5 0.0 copy-done.9
  310.5 11.2 %finish.5 = bf16[128,128,128]{2,1,0:T(8,128)(2,1)} custom-call(s32[2,512]{1,0:T(2,128)S(1)} %copy-done.9, bf16[104,64,128]{2,1,0:T(8,128)(2,1)} %last.5.mine_ref, bf16[104,64,128]{2,1,0:T(8,128)(2,1)} %copy-done.6, bf16[128,128,128]{2,1,0:T(8,128)(2,1)} %get-tuple-element.110.trunk_hbm.trunk_ref, s32[2,512]{1,0:T(2,128)S(1)} %copy-done.9, ...), custom_call_target="tpu_custom_call" | custom-call | tf_op jit(solution)/shard_map/cond/branch_1_fun/finish/pallas_call | solution.py:437
Async XLA Ops:
  111.3 3.9 %copy-start.13 = (bf16[2,64,64]{2,1,0:T(8,128)(2,1)S(1)}, bf16[2,64,64]{2,1,0:T(8,128)(2,1)}, u32[]{:S(2)}) copy-start(bf16[2,64,64]{2,1,0:T(8,128)(2,1)} %get-tuple-element.117) | copy-start | bytes 49156 | tf_op jit(solution)/shard_map/cond
  111.3 39.6 %all-to-all-start.5 = ((bf16[16,4,104,128]{3,2,1,0:T(8,128)(2,1)}), bf16[16,4,104,128]{3,2,1,0:T(8,128)(2,1)S(1)}, u32[]{:S(2)}, u32[]{:S(2)}) async-start(bf16[16,4,104,128]{3,2,1,0:T(8,128)(2,1)} %outgoing.5), calls=%async_computation.5 | async-start | bytes 3407872 | tf_op jit(solution)/shard_map/cond/branch_1_fun/all_to_all | solution.py:386
  150.9 1.2 copy-start.2
  297.8 7.7 %copy-start.17 = (bf16[128,64]{0,1:T(8,128)(2,1)S(1)}, bf16[128,64]{0,1:T(8,128)(2,1)}, u32[]{:S(2)}) copy-start(bf16[128,64]{0,1:T(8,128)(2,1)} %get-tuple-element.174) | copy-start | bytes 49156 | tf_op jit(solution)/shard_map/cond
  297.8 12.7 %copy-start.9 = (s32[2,512]{1,0:T(2,128)S(1)}, s32[2,512]{1,0:T(2,128)}, u32[]{:S(2)}) copy-start(s32[2,512]{1,0:T(2,128)} %get-tuple-element.106.cover_ref.cover_all_ref) | copy-start | bytes 12292 | tf_op jit(solution)/shard_map/cond
  305.5 3.8 %collective-permute-start.1 = (bf16[104,64,128]{2,1,0:T(8,128)(2,1)}, bf16[104,64,128]{2,1,0:T(8,128)(2,1)S(1)}, u32[]{:S(2)}, u32[]{:S(2)}) collective-permute-start(bf16[104,64,128]{2,1,0:T(8,128)(2,1)} %last.5.mine_ref), channel_id=1, source_target_pairs={{0,16},{16,0},{1,17},{17,1},{2,18},{18,2},{3,19},{19,3},{4,20},{20... | collective-permute-start | bytes 5111816 | tf_op jit(solution)/shard_map/cond/branch_1_fun/ppermute | solution.py:436
  309.3 1.2 copy-start.6
where the time goes:
time: 323 us; the launch traced here: 322 us
  blocking collectives  216 us (67%)
  Pallas kernels  53.8 us (17%)
  waiting for transfers between devices  38.2 us (12%)
  local copies, waits for them, and re-layouts  7.4 us (2%)
  starting transfers between devices  3.85 us (1%)
    all_to_all x3, blocking collectives, exchange(): return lax.all_to_all(values, ('row', 'col'), 0, 0, tiled=True)  216 us
    all_to_all x1, waiting for transfers between devices, exchange(): return lax.all_to_all(values, ('row', 'col'), 0, 0, tiled=True)  35.1 us
    pallas_call x1, Pallas kernels, with_capacity(): pl.pallas_call(functools.partial(pre_kernel, unit), grid=grid, in_specs=[...  14.1 us
    pallas_call x1, Pallas kernels, with_capacity(): pl.pallas_call(functools.partial(finish_kernel, unit), grid=(unit // GROU...  11.2 us
    pallas_call x1, Pallas kernels, with_capacity(): pl.pallas_call(functools.partial(mid_kernel, unit), grid=grid, in_specs=[...  10.9 us
    pallas_call x2, Pallas kernels, triangle(): pl.pallas_call(functools.partial(triangle_kernel, contract, rows_n, cols_...  9.95 us
    pallas_call x1, Pallas kernels, with_capacity(): pl.pallas_call(last_kernel, grid=grid, in_specs=[tri_spec, rep_spec, rep_...  7.67 us
  transfers between devices with their start and end apart: 2, of which 2 were waited for; matrix products, arithmetic and copies ran while one was open for 0% of the time, Pallas kernels for 0%

commit v1 on v0

--- a/solution.py
+++ b/solution.py
@@ -46,13 +46,54 @@
             gate_ref[at] = sigmoid(p[4]).astype(gate_ref.dtype)
 
 
-def store_by_channel(scratch, pair_ref):
-    slots, _, per_slot = pair_ref.shape[:3]
+def packing(capacity, unit, width, per_slot):
+    if unit == width:
+        for q, p in ((4, 3), (8, 7)):
+            if capacity * q <= width * p and 2 * per_slot % q == 0:
+                return q, p
+    return 1, 1
+
+
+def lanes_of(shape, dtype=jnp.int32):
+    return lax.broadcasted_iota(dtype, shape, len(shape) - 1)
+
+
+def pack(units, q, p):
+    if q == 1:
+        return units
+    width = units[0].shape[-1]
+    kept, piece = width // q * p, width // q
+    free = lanes_of(units[0].shape) >= kept
+    out = []
+    for first in range(0, len(units), q):
+        last = units[first + q - 1]
+        for e in range(p):
+            out.append(jnp.where(free, pltpu.roll(last, kept - e * piece, 1), units[first + e]))
+    return out
+
+
+def unpack_last(packed, q, p):
+    width = packed[0].shape[-1]
+    piece = width // q
+    at = lanes_of(packed[0].shape) // piece
+    out = jnp.zeros_like(packed[0])
+    for e in range(p):
+        out = jnp.where(at == e, pltpu.roll(packed[e], (e + 1) * piece, 1), out)
+    return out
+
+
+def store_by_channel(q, p, scratch, pair_ref):
+    slots, units = pair_ref.shape[:2]
+    per_slot = units // p * q // 2
     channels = slots * per_slot
-    for side in range(2):
-        for channel in range(channels):
-            rows = scratch[side, pl.ds(channel, GROUP, stride=channels + PAD), :]
-            pair_ref[channel // per_slot, side, channel % per_slot] = rows.astype(BF16)
+    for slot in range(slots):
+        values = [
+            scratch[side, pl.ds(slot * per_slot + channel, GROUP, stride=channels + PAD), :]
+            for side in range(2)
+            for channel in range(per_slot)
+        ]
+        for n, value in enumerate(pack(values, q, p)):
+            pair_ref[slot, n] = value.astype(BF16)
 
 
 STEP = 16
@@ -90,7 +131,7 @@
     return out
 
 
-def pre_kernel(unit, cover_ref, chain_ref, counts_ref, tp_hbm, trunk_hbm, cover_all_ref, chain_all_ref, chain_vec_ref,
+def pre_kernel(unit, q, p, cover_ref, chain_ref, counts_ref, tp_hbm, trunk_hbm, cover_all_ref, chain_all_ref, chain_vec_ref,
                trunk_weights_ref, weights_ref, pair_ref, rep_ref, gate_ref,
                scratch, tp_buffer, trunk_buffer, order, pick, sems):
     step_id = pl.program_id(0)
@@ -163,7 +204,7 @@
         return carry
 
     lax.fori_loop(0, GROUP // STEP, body, 0)
-    store_by_channel(scratch, pair_ref)
+    store_by_channel(q, p, scratch, pair_ref)
 
 
 def load_tri(tri_ref, tri_scratch):
@@ -202,7 +243,7 @@
     ]
 
 
-def mid_kernel(unit, counts_ref, tri_ref, rep_in_ref, gate_in_ref, out_weights_ref, weights_ref,
+def mid_kernel(unit, q, p, counts_ref, tri_ref, rep_in_ref, gate_in_ref, out_weights_ref, weights_ref,
                pair_ref, rep_ref, gate_ref, scratch, tri_scratch):
     base = pl.program_id(0) * GROUP
     load_tri(tri_ref, tri_scratch)
@@ -220,7 +261,7 @@
         return carry
 
     lax.fori_loop(0, GROUP // STEP, body, 0)
-    store_by_channel(scratch, pair_ref)
+    store_by_channel(q, p, scratch, pair_ref)
 
 
 def last_kernel(tri_ref, rep_in_ref, gate_in_ref, out_weights_ref, pooled_ref, tri_scratch):
@@ -291,24 +332,51 @@
     lax.fori_loop(0, GROUP // STEP, body, 0)
 
 
-def gather_sides(rows_n, cols_n, unit, pair_ref, sides):
-    height, width = pair_ref.shape[3:]
-
-    @pl.when(pl.program_id(0) == 0)
+def gather_sides(rows_n, cols_n, unit, q, p, pair_ref, sides):
+    units, height, width = pair_ref.shape[1:]
+    per_slot = units // p * q // 2
+    channel = pl.program_id(0)
+
+    @pl.when(channel == 0)
     def _():
         if height < unit:
             sides[...] = jnp.zeros_like(sides)
 
+    keep = (lanes_of((1, width)) < width // q * p).astype(F32).astype(BF16)
     for side in range(2):
-        for r in range(rows_n):
-            for c in range(cols_n):
-                sides[side, r * unit : r * unit + height, c * width : (c + 1) * width] = pair_ref[
-                    r * cols_n + c, side, 0
-                ]
-
-
-def triangle_kernel(contract, rows_n, cols_n, unit, pair_ref, tri_ref, sides):
-    gather_sides(rows_n, cols_n, unit, pair_ref, sides)
+        index = side * per_slot + channel
+        first = index // q * p
+
+        def fill(block, side=side):
+            def fill_rows(r, carry):
+                rows = pl.ds(pl.multiple_of(r * unit, unit), height)
+                for c in range(cols_n):
+                    sides[side, rows, c * width : (c + 1) * width] = block(r * cols_n + c)
+                return carry
+
+            lax.fori_loop(0, rows_n, fill_rows, 0)
+
+        if q == 1:
+            fill(lambda slot, index=index: pair_ref[slot, index])
+            continue
+
+        @pl.when(lax.rem(index, q) < p)
+        def _(fill=fill, index=index, first=first):
+            fill(lambda slot: pair_ref[slot, first + lax.rem(index, q)] * keep)
+
+        if (side + 1) * per_slot % q == 0:
+
+            @pl.when(lax.rem(index, q) == p)
+            def _(fill=fill, first=first):
+                fill(
+                    lambda slot: unpack_last(
+                        [pair_ref[slot, first + e].astype(F32) for e in range(p)], q, p
+                    ).astype(BF16)
+                )
+
+
+def triangle_kernel(contract, rows_n, cols_n, unit, q, p, pair_ref, tri_ref, sides):
+    gather_sides(rows_n, cols_n, unit, q, p, pair_ref, sides)
     out = lax.dot_general(
         sides[0], sides[1], (((contract,), (contract,)), ((), ())), preferred_element_type=F32
     )
@@ -320,12 +388,13 @@
             ].astype(BF16)
 
 
-def triangle(contract, rows_n, cols_n, unit, pairs, name):
-    slots, _, per_slot, height, width = pairs.shape
+def triangle(contract, rows_n, cols_n, unit, q, p, pairs, name):
+    slots, units, height, width = pairs.shape
+    per_slot = units // p * q // 2
     return pl.pallas_call(
-        functools.partial(triangle_kernel, contract, rows_n, cols_n, unit),
+        functools.partial(triangle_kernel, contract, rows_n, cols_n, unit, q, p),
         grid=(per_slot,),
-        in_specs=[pl.BlockSpec((slots, 2, 1, height, width), lambda c: (0, 0, c, 0, 0))],
+        in_specs=[pl.BlockSpec(pairs.shape, lambda c: (0, 0, 0, 0))],
         out_specs=pl.BlockSpec((slots, 1, height, width), lambda c: (0, c, 0, 0)),
         out_shape=jax.ShapeDtypeStruct((slots, per_slot, height, width), BF16),
         scratch_shapes=[pltpu.VMEM((2, rows_n * unit, cols_n * width), BF16)],
@@ -370,8 +439,10 @@
     chain_all = chain_ids[None]
     chain_column = chain_vec[:, None]
 
-    pair_spec = pl.BlockSpec((slots, 2, per_slot, GROUP, tile_cols), lambda g: (0, 0, 0, g, 0))
-    pair_shape = jax.ShapeDtypeStruct((slots, 2, per_slot, capacity, tile_cols), BF16)
+    q, p = packing(capacity, unit, tile_cols, per_slot)
+    units = 2 * per_slot // q * p
+    pair_spec = pl.BlockSpec((slots, units, GROUP, tile_cols), lambda g: (0, 0, g, 0))
+    pair_shape = jax.ShapeDtypeStruct((slots, units, capacity, tile_cols), BF16)
     rep_spec = rows_block(channels, tile_cols)
     rep_shape = jax.ShapeDtypeStruct((capacity, channels, tile_cols), BF16)
     trunk_spec = rows_block(trunk_channels, tile_cols)
@@ -386,7 +457,7 @@
         return lax.all_to_all(values, ("row", "col"), 0, 0, tiled=True)
 
     pairs, rep, gate = pl.pallas_call(
-        functools.partial(pre_kernel, unit),
+        functools.partial(pre_kernel, unit, q, p),
         grid=grid,
         in_specs=[
             SMEM,
@@ -412,9 +483,9 @@
         **gated_outs,
     )(coverage, chain_ids, counts, template_pair, trunk, coverage, chain_all, chain_column, trunk_weights, stacked[0])
 
-    tri = exchange(triangle(1, rows_n, cols_n, unit, exchange(pairs), "outgoing"))
+    tri = exchange(triangle(1, rows_n, cols_n, unit, q, p, exchange(pairs), "outgoing"))
     pairs, rep, gate = pl.pallas_call(
-        functools.partial(mid_kernel, unit),
+        functools.partial(mid_kernel, unit, q, p),
         grid=grid,
         in_specs=[SMEM, tri_spec, rep_spec, rep_spec, whole_block(out_weights[0]), whole_block(stacked[1])],
         scratch_shapes=[scratch, tri_scratch],
@@ -422,7 +493,7 @@
         **gated_outs,
     )(counts, tri.reshape(channels, capacity, tile_cols), rep, gate, out_weights[0], stacked[1])
 
-    tri = exchange(triangle(0, rows_n, cols_n, unit, exchange(pairs), "incoming"))
+    tri = exchange(triangle(0, rows_n, cols_n, unit, q, p, exchange(pairs), "incoming"))
     pooled = pl.pallas_call(
         last_kernel,
         grid=grid,

time: 323 us -> 307 us (0.950)
  blocking collectives: 216 us -> 197 us
    all_to_all x3, blocking collectives: 216 us -> 197 us  [exchange(): return lax.all_to_all(values, ('row', 'col'), 0, 0, tiled=True)]
where the time goes in v1:
time: 307 us; the launch traced here: 306 us
  blocking collectives  197 us (64%)
  Pallas kernels  56.8 us (19%)
  waiting for transfers between devices  38.2 us (12%)
  local copies, waits for them, and re-layouts  7.4 us (2%)
  starting transfers between devices  3.85 us (1%)
    all_to_all x3, blocking collectives, exchange(): return lax.all_to_all(values, ('row', 'col'), 0, 0, tiled=True)  197 us
    all_to_all x1, waiting for transfers between devices, exchange(): return lax.all_to_all(values, ('row', 'col'), 0, 0, tiled=True)  35.1 us
    pallas_call x1, Pallas kernels, with_capacity(): pl.pallas_call(functools.partial(pre_kernel, unit, q, p), grid=grid, in_s...  14.3 us
    pallas_call x2, Pallas kernels, triangle(): pl.pallas_call(functools.partial(triangle_kernel, contract, rows_n, cols_...  12.9 us
    pallas_call x1, Pallas kernels, with_capacity(): pl.pallas_call(functools.partial(finish_kernel, unit), grid=(unit // GROU...  11.2 us
    pallas_call x1, Pallas kernels, with_capacity(): pl.pallas_call(functools.partial(mid_kernel, unit, q, p), grid=grid, in_s...  10.8 us
    pallas_call x1, Pallas kernels, with_capacity(): pl.pallas_call(last_kernel, grid=grid, in_specs=[tri_spec, rep_spec, rep_...  7.67 us
  transfers between devices with their start and end apart: 2, of which 2 were waited for; matrix products, arithmetic and copies ran while one was open for 0% of the time, Pallas kernels for 0%

profile of v1, /device:TPU:0, one launch (start us, length us, event | category | flops | bytes accessed | tf_op | source)
XLA Modules:
  0.0 305.5 jit_solution(14687827868828019793)
XLA Ops:
  0.0 0.7 reshape.47
  0.7 0.1 reduce_sum.9
  0.8 0.6 reduce_max.9
  3.4 302.1 %conditional.1 = (bf16[128,128,128]{2,1,0:T(8,128)(2,1)}) conditional(s32[]{:T(128)} %clamp.3, (s32[512]{0:T(512)}, f32[64]{0:T(128)}, bf16[2,5,64,64]{3,2,1,0:T(8,128)(2,1)}, s32[2,512]{1,0:T(2,128)}, s32[2,4]{1,0:T(2,128)S(1)}, /*index=5*/bf16[1,128,64,128]{3,2,1,0:T(8,128)(2,1)}, bf16[128,128,128]{2,1,0:T(8,128)(2,1)}, ...), branch_computations={%region_2.0_spmd, %region_3.0_spmd, %region_4.0_spmd, %region_5.0_... | conditional | bytes 52806364 | solution.py:538
  3.4 1.6 fusion.1
  5.0 1.4 copy.15.chain_vec_ref
  6.4 14.3 %pre.5 = (bf16[16,7,104,128]{3,2,1,0:T(8,128)(2,1)}, bf16[104,64,128]{2,1,0:T(8,128)(2,1)}, bf16[104,64,128]{2,1,0:T(8,128)(2,1)}) custom-call(s32[2,512]{1,0:T(2,128)} %get-tuple-element.106.cover_ref.cover_all_ref, s32[512]{0:T(512)} %get-tuple-element.108.chain_ref, s32[2,4]{1,0:T(2,128)S(1)} %get-tuple-element.107.counts_ref, ...), custom_call_target="tpu_custom_call" | custom-call | tf_op jit(solution)/shard_map/cond/branch_1_fun/pre/pallas_call | solution.py:459
  20.6 76.6 %all_to_all.67.pair_ref = bf16[16,7,104,128]{3,2,1,0:T(8,128)(2,1)} all-to-all(bf16[16,7,104,128]{3,2,1,0:T(8,128)(2,1)} %get-tuple-element.114), channel_id=1, replica_groups=mesh['tmpl'=2,'row'=4,'col'=4] {'row','col'}, dimensions={0} | all-to-all | bytes 5963776 | tf_op jit(solution)/shard_map/cond/branch_1_fun/all_to_all | solution.py:457
  97.2 6.4 %outgoing.5 = bf16[16,4,104,128]{3,2,1,0:T(8,128)(2,1)} custom-call(bf16[16,7,104,128]{3,2,1,0:T(8,128)(2,1)} %all_to_all.67.pair_ref), custom_call_target="tpu_custom_call" | custom-call | tf_op jit(solution)/shard_map/cond/branch_1_fun/outgoing/pallas_call | solution.py:394
  103.7 0.0 copy-start.13
  103.7 3.8 %all-to-all-start.5 = ((bf16[16,4,104,128]{3,2,1,0:T(8,128)(2,1)}), bf16[16,4,104,128]{3,2,1,0:T(8,128)(2,1)S(1)}, u32[]{:S(2)}, u32[]{:S(2)}) async-start(bf16[16,4,104,128]{3,2,1,0:T(8,128)(2,1)} %outgoing.5), calls=%async_computation.5 | async-start | bytes 3407872 | tf_op jit(solution)/shard_map/cond/branch_1_fun/all_to_all | solution.py:457
  107.5 0.0 copy-done.13
  107.5 0.6 slice_bitcast_fusion.2
  108.1 35.1 %all-to-all-done.5 = bf16[16,4,104,128]{3,2,1,0:T(8,128)(2,1)S(1)} async-done(((bf16[16,4,104,128]{3,2,1,0:T(8,128)(2,1)}), bf16[16,4,104,128]{3,2,1,0:T(8,128)(2,1)S(1)}, u32[]{:S(2)}, u32[]{:S(2)}) %all-to-all-start.5) | async-done | bytes 1703968 | tf_op jit(solution)/shard_map/cond/branch_1_fun/all_to_all | solution.py:457
  143.2 0.0 copy-start.2
  143.2 1.2 copy-done.2
  144.5 10.8 %mid.5 = (bf16[16,7,104,128]{3,2,1,0:T(8,128)(2,1)}, bf16[104,64,128]{2,1,0:T(8,128)(2,1)}, bf16[104,64,128]{2,1,0:T(8,128)(2,1)}) custom-call(s32[2,4]{1,0:T(2,128)S(1)} %get-tuple-element.107.counts_ref, bf16[64,104,128]{2,1,0:T(8,128)(2,1)} %bitcast.44, bf16[104,64,128]{2,1,0:T(8,128)(2,1)} %get-tuple-element.115.rep_in_ref, ...), custom_call_target="tpu_custom_call" | custom-call | tf_op jit(solution)/shard_map/cond/branch_1_fun/mid/pallas_call | solution.py:487
  155.3 75.6 %all_to_all.68.pair_ref = bf16[16,7,104,128]{3,2,1,0:T(8,128)(2,1)} all-to-all(bf16[16,7,104,128]{3,2,1,0:T(8,128)(2,1)} %get-tuple-element.118), channel_id=1, replica_groups=mesh['tmpl'=2,'row'=4,'col'=4] {'row','col'}, dimensions={0} | all-to-all | bytes 5963776 | tf_op jit(solution)/shard_map/cond/branch_1_fun/all_to_all | solution.py:457
  230.9 6.4 %incoming.5 = bf16[16,4,104,128]{3,2,1,0:T(8,128)(2,1)} custom-call(bf16[16,7,104,128]{3,2,1,0:T(8,128)(2,1)} %all_to_all.68.pair_ref), custom_call_target="tpu_custom_call" | custom-call | tf_op jit(solution)/shard_map/cond/branch_1_fun/incoming/pallas_call | solution.py:394
  237.3 44.4 %all_to_all.69 = bf16[16,4,104,128]{3,2,1,0:T(8,128)(2,1)} all-to-all(bf16[16,4,104,128]{3,2,1,0:T(8,128)(2,1)} %incoming.5), channel_id=1, replica_groups=mesh['tmpl'=2,'row'=4,'col'=4] {'row','col'}, dimensions={0} | all-to-all | bytes 3407872 | tf_op jit(solution)/shard_map/cond/branch_1_fun/all_to_all | solution.py:457
  281.7 0.0 copy-start.17
  281.7 0.0 copy-start.9
  281.7 7.7 %last.5.mine_ref = bf16[104,64,128]{2,1,0:T(8,128)(2,1)} custom-call(bf16[64,104,128]{2,1,0:T(8,128)(2,1)} %bitcast.45, bf16[104,64,128]{2,1,0:T(8,128)(2,1)} %get-tuple-element.119.rep_in_ref, bf16[104,64,128]{2,1,0:T(8,128)(2,1)} %get-tuple-element.120.gate_in_ref, bf16[64,64]{1,0:T(8,128)(2,1)} %get-tuple-element.201.out_weights_ref), custom_call_target="tpu_custom_call" | custom-call | tf_op jit(solution)/shard_map/cond/branch_1_fun/last/pallas_call | solution.py:497
  289.4 0.0 collective-permute-start.1
  289.4 0.0 copy-done.17
  289.4 0.7 copy.19.final_weights_ref
  290.1 3.1 %collective-permute-done.1.other_ref = bf16[104,64,128]{2,1,0:T(8,128)(2,1)S(1)} collective-permute-done((bf16[104,64,128]{2,1,0:T(8,128)(2,1)}, bf16[104,64,128]{2,1,0:T(8,128)(2,1)S(1)}, u32[]{:S(2)}, u32[]{:S(2)}) %collective-permute-start.1) | collective-permute-done | bytes 1703968 | tf_op jit(solution)/shard_map/cond/branch_1_fun/ppermute | solution.py:507
  293.2 0.0 copy-start.6
  293.2 1.2 copy-done.6
  294.4 0.0 copy-done.9
  294.4 11.2 %finish.5 = bf16[128,128,128]{2,1,0:T(8,128)(2,1)} custom-call(s32[2,512]{1,0:T(2,128)S(1)} %copy-done.9, bf16[104,64,128]{2,1,0:T(8,128)(2,1)} %last.5.mine_ref, bf16[104,64,128]{2,1,0:T(8,128)(2,1)} %copy-done.6, bf16[128,128,128]{2,1,0:T(8,128)(2,1)} %get-tuple-element.110.trunk_hbm.trunk_ref, s32[2,512]{1,0:T(2,128)S(1)} %copy-done.9, ...), custom_call_target="tpu_custom_call" | custom-call | tf_op jit(solution)/shard_map/cond/branch_1_fun/finish/pallas_call | solution.py:508
Async XLA Ops:
  103.7 3.9 %copy-start.13 = (bf16[2,64,64]{2,1,0:T(8,128)(2,1)S(1)}, bf16[2,64,64]{2,1,0:T(8,128)(2,1)}, u32[]{:S(2)}) copy-start(bf16[2,64,64]{2,1,0:T(8,128)(2,1)} %get-tuple-element.117) | copy-start | bytes 49156 | tf_op jit(solution)/shard_map/cond
  103.7 39.6 %all-to-all-start.5 = ((bf16[16,4,104,128]{3,2,1,0:T(8,128)(2,1)}), bf16[16,4,104,128]{3,2,1,0:T(8,128)(2,1)S(1)}, u32[]{:S(2)}, u32[]{:S(2)}) async-start(bf16[16,4,104,128]{3,2,1,0:T(8,128)(2,1)} %outgoing.5), calls=%async_computation.5 | async-start | bytes 3407872 | tf_op jit(solution)/shard_map/cond/branch_1_fun/all_to_all | solution.py:457
  143.2 1.2 copy-start.2
  281.7 7.7 %copy-start.17 = (bf16[128,64]{0,1:T(8,128)(2,1)S(1)}, bf16[128,64]{0,1:T(8,128)(2,1)}, u32[]{:S(2)}) copy-start(bf16[128,64]{0,1:T(8,128)(2,1)} %get-tuple-element.174) | copy-start | bytes 49156 | tf_op jit(solution)/shard_map/cond
  281.7 12.7 %copy-start.9 = (s32[2,512]{1,0:T(2,128)S(1)}, s32[2,512]{1,0:T(2,128)}, u32[]{:S(2)}) copy-start(s32[2,512]{1,0:T(2,128)} %get-tuple-element.106.cover_ref.cover_all_ref) | copy-start | bytes 12292 | tf_op jit(solution)/shard_map/cond
  289.4 3.8 %collective-permute-start.1 = (bf16[104,64,128]{2,1,0:T(8,128)(2,1)}, bf16[104,64,128]{2,1,0:T(8,128)(2,1)S(1)}, u32[]{:S(2)}, u32[]{:S(2)}) collective-permute-start(bf16[104,64,128]{2,1,0:T(8,128)(2,1)} %last.5.mine_ref), channel_id=1, source_target_pairs={{0,16},{16,0},{1,17},{17,1},{2,18},{18,2},{3,19},{19,3},{4,20},{20... | collective-permute-start | bytes 5111816 | tf_op jit(solution)/shard_map/cond/branch_1_fun/ppermute | solution.py:507
  293.2 1.2 copy-start.6
